TPU v7x, 32 devices: a whole 2x2x4 slice. The times are simulated.
32 devices in a mesh: role: 2 (over x), gy: 2 (over y), gx: 8 (over z, core).
Axes of the slice: x: 2, y: 2, z: 4, core: 2. Of those that a mesh axis runs over, the one named last changes fastest.
Arguments:
- thermal_anomaly: float32 [16, 192, 2048], P('role', 'gy', 'gx'), may hold values from -6 to 6
- saltiness_anomaly: float32 [16, 192, 2048], P('role', 'gy', 'gx'), may hold values from -6 to 6
- zonal_flow_fraction: bfloat16 [16, 192, 2048], P('role', 'gy', 'gx'), may hold values from -0.5 to 0.5
- meridional_flow_fraction: bfloat16 [16, 192, 2048], P('role', 'gy', 'gx'), may hold values from -0.5 to 0.5
- mixing_coefficient: float32 [16], P('role'), may hold values from 0.03 to 0.2
- continent_patch_numbering: int32 [2], replicated, may hold values from 0 to 15
- parallel_band_coefficients: bfloat16 [16, 4, 12], P('gy'), may hold values from -1.75 to 1.75
- meridian_panel_coefficients: bfloat16 [14, 512, 128], replicated, may hold values from -0.25 to 0.25
- panel_starting_source_meridian: int32 [14], replicated, may hold values from 0 to 1536, as said below
- target_parallel_cluster: int32 [64], replicated, may hold values from 0 to 7, as said below
Outputs:
- remapped: bfloat16 [3, 16, 64, 1792], P(None, 'role', ('gy', 'gx'))
- checksums: float32 [3, 8], replicated
Inputs may be any that keep to these rules, and one draw needn't show every extreme that they name: `panel_starting_source_meridian`: every block's window lies within the model grid. `target_parallel_cluster`: each group number names exactly 8 rows.
All inputs are finite; a program needn't handle non-finite values.
Results may differ from a plain program's by a relative error of at most 0.0057.
Values may be sent and summed in bfloat16 or wider, within the bound.
A program may use at most 64 MiB of HBM per device.

v0:
```python
import math

import jax
import jax.numpy as jnp
from jax import lax
from jax.sharding import PartitionSpec as P


def with_halo(cells, sides, width):
    for axis, dim in sides:
        count = lax.axis_size(axis)
        head = lax.slice_in_dim(cells, 0, width, axis=dim)
        tail = lax.slice_in_dim(cells, cells.shape[dim] - width, cells.shape[dim], axis=dim)
        cells = jnp.concatenate(
            [
                lax.ppermute(tail, axis, [(i, (i + 1) % count) for i in range(count)]),
                cells,
                lax.ppermute(head, axis, [((i + 1) % count, i) for i in range(count)]),
            ],
            axis=dim,
        )
    return cells


def advance(padded, east_speed, north_speed, kappa, ocean):
    centre = padded[:, :, 1:-1, 1:-1]
    east = padded[:, :, 1:-1, 2:]
    west = padded[:, :, 1:-1, :-2]
    north = padded[:, :, 2:, 1:-1]
    south = padded[:, :, :-2, 1:-1]
    tendency = (
        -east_speed * (east - west) * 0.5
        - north_speed * (north - south) * 0.5
        + kappa * (east + west + north + south - 4.0 * centre)
    )
    return centre + ocean * tendency


def clear_outside(padded, mesh_zonal_extent):
    mesh_meridional_extent = padded.shape[2]
    first = (
        lax.axis_index("gy") * (mesh_meridional_extent - 2 * mesh_zonal_extent) - mesh_zonal_extent
    )
    global_rows = first + lax.broadcasted_iota(jnp.int32, (mesh_meridional_extent, 1), 0)
    inside = (global_rows >= 0) & (
        global_rows < (mesh_meridional_extent - 2 * mesh_zonal_extent) * lax.axis_size("gy")
    )
    return padded * inside.astype(padded.dtype)


def tile_table(continent_patch_numbering):
    count_y = lax.axis_size("gy")
    count_x = lax.axis_size("gx")
    shifts = jnp.arange(3, dtype=jnp.int32) - 1
    tile_rows = jnp.clip(lax.axis_index("gy") + shifts, 0, count_y - 1)
    tile_cols = (lax.axis_index("gx") + shifts) % count_x
    numbers = tile_rows[:, None] * count_x + tile_cols[None, :]
    listed = jnp.any(numbers[:, :, None] == continent_patch_numbering[None, None, :], axis=2)
    return 1.0 - listed.astype(jnp.float32)


def density(temp, salt, level):
    return 0.78 * salt - 0.17 * temp * (1.0 + 0.03 * level) - 0.02 * temp * temp


def lon_remap(lat_out, meridian_panel_coefficients, panel_starting_source_meridian):
    block_count, source_width, block_width = meridian_panel_coefficients.shape
    leading = lat_out.shape[:3]
    flat = lat_out.reshape(-1, lat_out.shape[3])

    def one_block(index, result):
        start = panel_starting_source_meridian[index]
        window = lax.dynamic_slice_in_dim(flat, start, source_width, 1)
        weights = lax.dynamic_index_in_dim(meridian_panel_coefficients, index, 0, keepdims=False)
        product = jnp.dot(window, weights, preferred_element_type=jnp.float32)
        return lax.dynamic_update_slice_in_dim(result, product, index * block_width, 1)

    empty = jnp.zeros((flat.shape[0], block_count * block_width), jnp.float32)
    result = lax.fori_loop(0, block_count, one_block, empty)
    return result.reshape(leading + (block_count * block_width,))


def rim(scalar_field_pair):
    padded = with_halo(scalar_field_pair, (("gy", 2), ("gx", 3)), 1)
    return clear_outside(padded, 1)


def body(
    thermal_anomaly,
    saltiness_anomaly,
    zonal_flow_fraction,
    meridional_flow_fraction,
    mixing_coefficient,
    continent_patch_numbering,
    parallel_band_coefficients,
    meridian_panel_coefficients,
    panel_starting_source_meridian,
    target_parallel_cluster,
):
    vertical_layer_number, mesh_meridional_extent, mesh_zonal_extent = thermal_anomaly.shape
    east_speed = zonal_flow_fraction.astype(jnp.float32)
    north_speed = meridional_flow_fraction.astype(jnp.float32)
    kappa = mixing_coefficient[:, None, None]
    level = (
        lax.axis_index("role") * vertical_layer_number
        + jnp.arange(vertical_layer_number, dtype=jnp.int32)
    ).astype(jnp.float32)
    table = tile_table(continent_patch_numbering)
    own_flag = table[1, 1]
    scalar_field_pair = jnp.stack([thermal_anomaly, saltiness_anomaly])
    first = advance(rim(scalar_field_pair), east_speed, north_speed, kappa, own_flag)
    second = advance(rim(first), east_speed, north_speed, kappa, own_flag)
    level_b = level[:, None, None]
    fields_one = jnp.stack([first[0], first[1], density(first[0], first[1], level_b)])
    fields_two = jnp.stack([second[0], second[1], density(second[0], second[1], level_b)])
    means = ((fields_one + fields_two) * 0.5).astype(jnp.bfloat16)
    count_x = lax.axis_size("gx")
    strips = means.reshape(
        3, vertical_layer_number, count_x, mesh_meridional_extent // count_x, mesh_zonal_extent
    )
    lat_out = jnp.einsum(
        "gts,flgsx->flgtx", parallel_band_coefficients, strips, preferred_element_type=jnp.float32
    )
    lat_out = lat_out.astype(jnp.bfloat16).reshape(
        3, vertical_layer_number, count_x * parallel_band_coefficients.shape[1], mesh_zonal_extent
    )
    values = lon_remap(
        lax.all_to_all(lat_out, "gx", split_axis=2, concat_axis=3, tiled=True),
        meridian_panel_coefficients,
        panel_starting_source_meridian,
    )
    out_rows = parallel_band_coefficients.shape[1]
    total_rows = out_rows * lax.axis_size("gy") * count_x
    groups = 4 * lax.axis_size("gy")
    thick = 1.0 + 0.25 * level
    quadratic_entries = jnp.sum(values * values, axis=3)
    weighted = jnp.sum(quadratic_entries * thick[None, :, None], axis=1)
    strip_index = lax.axis_index("gy") * count_x + lax.axis_index("gx")
    first_row = strip_index * out_rows
    all_rows = jnp.arange(total_rows, dtype=jnp.float32)
    area = jnp.cos((-75.0 + 150.0 * (all_rows + 0.5) / total_rows) * (math.pi / 180.0))
    own_area = lax.dynamic_slice_in_dim(area, first_row, out_rows)
    own_groups = lax.dynamic_slice_in_dim(target_parallel_cluster, first_row, out_rows)
    labels = jnp.arange(groups, dtype=jnp.int32)[None, :]
    own_hot = (own_groups[:, None] == labels).astype(jnp.float32)
    partial_value = jnp.dot(weighted * own_area[None, :], own_hot, precision=lax.Precision.HIGHEST)
    numer = lax.psum(partial_value, ("role", "gy", "gx"))
    full_hot = (target_parallel_cluster[:, None] == labels).astype(jnp.float32)
    all_levels = jnp.arange(vertical_layer_number * lax.axis_size("role"), dtype=jnp.float32)
    thick_total = jnp.sum(1.0 + 0.25 * all_levels)
    denom = thick_total * values.shape[3] * jnp.dot(area, full_hot, precision=lax.Precision.HIGHEST)
    return (values.astype(jnp.bfloat16), numer / denom[None, :])


def solution(mesh):
    in_specs = (
        P("role", "gy", "gx"),
        P("role", "gy", "gx"),
        P("role", "gy", "gx"),
        P("role", "gy", "gx"),
        P("role"),
        P(),
        P("gy", None, None),
        P(),
        P(),
        P(),
    )
    out_specs = (P(None, "role", ("gy", "gx"), None), P())
    return jax.shard_map(body, mesh=mesh, in_specs=in_specs, out_specs=out_specs, check_vma=False)
```

profile of v0, /device:TPU:0, one launch (start us, length us, event | category | flops | bytes accessed | tf_op | source)
XLA Modules:
  0.0 159.5 jit_solution(15695306317298125391)
XLA Ops:
  0.6 2.3 %copy_bitcast_fusion = (f32[1,8,96,256]{3,1,2,0:T(8,128)S(1)}, f32[1,8,96,256]{3,1,2,0:T(8,128)S(1)}) fusion(f32[8,96,256]{2,1,0:T(8,128)} %param.13, f32[8,96,256]{2,1,0:T(8,128)} %param.12), kind=kLoop, calls=%fused_computation.28 | loop fusion | bytes 3145728 | tf_op jit(solution)/shard_map/stack | solution.py:110
  3.0 3.1 %collective-permute-start = (f32[2,8,1,256]{3,1,2,0:T(8,128)S(1)}, f32[2,8,1,256]{3,1,2,0:T(8,128)S(1)}, u32[]{:S(2)}, u32[]{:S(2)}) collective-permute-start(f32[2,8,1,256]{3,1,2,0:T(8,128)S(1)} %get-tuple-element.113), channel_id=1, source_target_pairs={{0,8},{8,0},{1,9},{9,1},{2,10},{10,2},{3,11},{11,3},{4,12},{12,4},... | collective-permute-start | bytes 49160 | tf_op jit(solution)/shard_map/ppermute | solution.py:16
  7.9 1.9 %collective-permute-done.1 = f32[2,8,1,256]{3,1,2,0:T(8,128)S(1)} collective-permute-done((f32[2,8,1,256]{3,1,2,0:T(8,128)S(1)}, f32[2,8,1,256]{3,1,2,0:T(8,128)S(1)}, u32[]{:S(2)}, u32[]{:S(2)}) %collective-permute-start.1) | collective-permute-done | bytes 16416 | tf_op jit(solution)/shard_map/ppermute | solution.py:18
  12.1 3.5 %collective-permute-start.3 = (f32[2,8,98,1]{2,1,3,0:T(8,128)}, f32[2,8,98,1]{2,1,3,0:T(8,128)}, u32[]{:S(2)}, u32[]{:S(2)}) collective-permute-start(f32[2,8,98,1]{2,1,3,0:T(8,128)} %copy.49), channel_id=1, source_target_pairs={{1,0},{2,1},{3,2},{4,3},{5,4},{6,5},{7,6},{0,7},{9,8},{10,9},{11,1... | collective-permute-start | bytes 18824 | tf_op jit(solution)/shard_map/ppermute | solution.py:18
  16.1 1.2 slice.80
  17.3 1.6 copy.52
  19.2 1.9 %copy.50 = f32[2,8,98,1]{3,1,2,0:T(8,128)} copy(f32[2,8,98,1]{2,1,3,0:T(8,128)} %collective-permute-done.2) | data formatting | bytes 12544 | tf_op jit(solution)/shard_map/ppermute | solution.py:16
  21.2 2.0 %copy.51 = f32[2,8,98,1]{3,1,2,0:T(8,128)} copy(f32[2,8,98,1]{2,1,3,0:T(8,128)} %collective-permute-done.3) | data formatting | bytes 12544 | tf_op jit(solution)/shard_map/ppermute | solution.py:18
  23.2 2.4 %maximum_multiply_fusion = f32[2,8,98,258]{3,1,2,0:T(8,128)S(1)} fusion(f32[2,8,98,1]{3,1,2,0:T(8,128)} %copy.51, f32[2,8,1,256]{3,1,2,0:T(8,128)S(1)} %copy-done.6, f32[1,8,96,256]{3,1,2,0:T(8,128)S(1)} %get-tuple-element.119, f32[1,8,96,256]{3,1,2,0:T(8,128)S(1)} %get-tuple-element.120, f32[2,8,1,256]{3,1,2,0:T(8,128)S(1)} %copy-done.4, ...), kind=kLoop, calls=%fused_computation.5 | loop fusion | flops 2427264 | bytes 3236744 | tf_op jit(solution)/shard_map/mul | solution.py:48
  25.6 2.2 %multiply_add_fusion.1 = f32[2,8,96,256]{3,1,2,0:T(8,128)S(1)} fusion(f32[2,8,98,258]{3,1,2,0:T(8,128)S(1)} %maximum_multiply_fusion, f32[8]{0:T(128)S(1)} %copy-done.7, f32[8,96,256]{2,0,1:T(8,128)S(1)} %copy.53, f32[8,96,256]{2,0,1:T(8,128)S(1)} %copy.52, f32[]{:T(128)} %bitcast.4), kind=kLoop, calls=%fused_computation.15 | loop fusion | flops 6291456 | bytes 11010084 | tf_op jit(solution)/shard_map/add | solution.py:36
  28.5 1.4 collective-permute-start.5
  29.9 1.7 %collective-permute-done.4 = f32[2,8,1,256]{3,1,2,0:T(8,128)S(1)} collective-permute-done((f32[2,8,1,256]{3,1,2,0:T(8,128)S(1)}, f32[2,8,1,256]{3,1,2,0:T(8,128)S(1)}, u32[]{:S(2)}, u32[]{:S(2)}) %collective-permute-start.4) | collective-permute-done | bytes 16416 | tf_op jit(solution)/shard_map/ppermute | solution.py:16
  32.4 1.4 fusion.31
  33.8 1.4 copy.54
  35.3 1.4 copy.55
  36.7 3.7 %collective-permute-start.7 = (f32[2,8,98,1]{2,1,3,0:T(8,128)S(1)}, f32[2,8,98,1]{2,1,3,0:T(8,128)S(1)}, u32[]{:S(2)}, u32[]{:S(2)}) collective-permute-start(f32[2,8,98,1]{2,1,3,0:T(8,128)S(1)} %copy.55), channel_id=1, source_target_pairs={{1,0},{2,1},{3,2},{4,3},{5,4},{6,5},{7,6},{0,7},{9,8},{10,9},{11,1... | collective-permute-start | bytes 18824 | tf_op jit(solution)/shard_map/ppermute | solution.py:18
  40.4 1.3 copy.56
  41.8 1.3 copy.57
  43.0 2.4 %maximum_multiply_fusion.1 = f32[2,8,98,258]{3,1,2,0:T(8,128)S(1)} fusion(f32[2,8,98,1]{3,1,2,0:T(8,128)} %copy.57, f32[2,8,1,256]{3,1,2,0:T(8,128)S(1)} %collective-permute-done.5, f32[2,8,96,256]{3,1,2,0:T(8,128)S(1)} %multiply_add_fusion.1, f32[2,8,1,256]{3,1,2,0:T(8,128)S(1)} %collective-permute-done.4, f32[2,8,98,1]{3,1,2,0:T(8,128)} %copy.56, ...), kind=kLoop, calls=%fused_computation.6 | loop fusion | flops 2022720 | bytes 3236744 | tf_op jit(solution)/shard_map/mul | solution.py:48
  45.4 2.2 %multiply_add_fusion = f32[2,8,96,256]{3,1,2,0:T(8,128)S(1)} fusion(f32[2,8,98,258]{3,1,2,0:T(8,128)S(1)} %maximum_multiply_fusion.1, f32[8]{0:T(128)S(1)} %copy-done.7, f32[8,96,256]{2,0,1:T(8,128)S(1)} %copy.53, f32[8,96,256]{2,0,1:T(8,128)S(1)} %copy.52, f32[]{:T(128)} %bitcast.4), kind=kLoop, calls=%fused_computation.14 | loop fusion | flops 6291456 | bytes 11010084 | tf_op jit(solution)/shard_map/add | solution.py:36
  49.9 4.9 %all-to-all-start = ((bf16[3,8,32,256]{3,1,0,2:T(8,128)(2,1)}), bf16[3,8,32,256]{3,1,0,2:T(8,128)(2,1)S(1)}, u32[]{:S(2)}, u32[]{:S(2)}) async-start(bf16[3,8,32,256]{3,1,0,2:T(8,128)(2,1)} %bitcast.13), calls=%async_computation | async-start | bytes 786432 | tf_op jit(solution)/shard_map/all_to_all | solution.py:128
  56.5 10.8 %all-to-all-done = bf16[3,8,32,256]{3,1,0,2:T(8,128)(2,1)S(1)} async-done(((bf16[3,8,32,256]{3,1,0,2:T(8,128)(2,1)}), bf16[3,8,32,256]{3,1,0,2:T(8,128)(2,1)S(1)}, u32[]{:S(2)}, u32[]{:S(2)}) %all-to-all-start) | async-done | bytes 393248 | tf_op jit(solution)/shard_map/all_to_all | solution.py:128
  67.7 51.8 %while.13 = (s32[]{:T(128)}, f32[96,1792]{1,0:T(8,128)S(1)}, s32[14]{0:T(128)S(1)}, bf16[96,2048]{1,0:T(8,128)(2,1)S(1)}, bf16[14,512,128]{2,1,0:T(8,128)(2,1)},...) while((s32[]{:T(128)}, f32[96,1792]{1,0:T(8,128)S(1)}, s32[14]{0:T(128)S(1)}, ...), condition=%wide.region_2.3_spmd, body=%wide.region_1.2_spmd.sunk | while | flops 12582921 | bytes 279241 | solution.py:79
  120.9 38.0 %psum.7 = f32[3,8]{1,0:T(4,128)S(1)} all-reduce(f32[3,8]{1,0:T(4,128)S(1)} %fusion.21), channel_id=1, replica_groups=mesh['role'=2,'gy'=2,'gx'=8] {'role','gy','gx'}, use_global_device_ids=true, to_apply=%region_5.6 | all-reduce | flops 24 | bytes 192 | tf_op jit(solution)/shard_map/psum | solution.py:147
  (96 shorter events, 36.1 us)
Async XLA Ops:
  0.6 48.1 %copy-start = (bf16[8,4,12]{2,1,0:T(4,128)(2,1)S(1)}, bf16[8,4,12]{2,1,0:T(4,128)(2,1)}, u32[]{:S(2)}) copy-start(bf16[8,4,12]{2,1,0:T(4,128)(2,1)} %param.18) | copy-start | bytes 2308
  2.9 3.2 %copy-start.1 = (bf16[8,96,256]{2,1,0:T(8,128)(2,1)S(1)}, bf16[8,96,256]{2,1,0:T(8,128)(2,1)}, u32[]{:S(2)}) copy-start(bf16[8,96,256]{2,1,0:T(8,128)(2,1)} %param.14) | copy-start | bytes 1179652
  2.9 4.2 %copy-start.9 = (s32[2]{0:T(128)S(1)}, s32[2]{0:T(128)}, u32[]{:S(2)}) copy-start(s32[2]{0:T(128)} %param.17) | copy-start | bytes 28
  3.0 4.9 %collective-permute-start = (f32[2,8,1,256]{3,1,2,0:T(8,128)S(1)}, f32[2,8,1,256]{3,1,2,0:T(8,128)S(1)}, u32[]{:S(2)}, u32[]{:S(2)}) collective-permute-start(f32[2,8,1,256]{3,1,2,0:T(8,128)S(1)} %get-tuple-element.113), channel_id=1, source_target_pairs={{0,8},{8,0},{1,9},{9,1},{2,10},{10,2},{3,11},{11,3},{4,12},{12,4},... | collective-permute-start | bytes 49160 | tf_op jit(solution)/shard_map/ppermute | solution.py:16
  6.0 3.7 %collective-permute-start.1 = (f32[2,8,1,256]{3,1,2,0:T(8,128)S(1)}, f32[2,8,1,256]{3,1,2,0:T(8,128)S(1)}, u32[]{:S(2)}, u32[]{:S(2)}) collective-permute-start(f32[2,8,1,256]{3,1,2,0:T(8,128)S(1)} %get-tuple-element.114), channel_id=1, source_target_pairs={{8,0},{0,8},{9,1},{1,9},{10,2},{2,10},{11,3},{3,11},{12,4},{4,12},... | collective-permute-start | bytes 49160 | tf_op jit(solution)/shard_map/ppermute | solution.py:18
  7.8 1.9 %copy-start.3 = (f32[2,8,1,256]{3,1,2,0:T(8,128)}, f32[2,8,1,256]{3,1,2,0:T(8,128)S(1)}, u32[]{:S(2)}) copy-start(f32[2,8,1,256]{3,1,2,0:T(8,128)S(1)} %collective-permute-done) | copy-start | bytes 49156
  9.8 0.6 copy-start.5
  11.1 7.9 %copy-start.2 = (bf16[8,96,256]{2,1,0:T(8,128)(2,1)S(1)}, bf16[8,96,256]{2,1,0:T(8,128)(2,1)}, u32[]{:S(2)}) copy-start(bf16[8,96,256]{2,1,0:T(8,128)(2,1)} %param.15) | copy-start | bytes 1179652
  11.1 8.1 %collective-permute-start.2 = (f32[2,8,98,1]{2,1,3,0:T(8,128)S(1)}, f32[2,8,98,1]{2,1,3,0:T(8,128)}, u32[]{:S(2)}, u32[]{:S(2)}) collective-permute-start(f32[2,8,98,1]{2,1,3,0:T(8,128)S(1)} %copy.48), channel_id=1, source_target_pairs={{0,1},{1,2},{2,3},{3,4},{4,5},{5,6},{6,7},{7,0},{8,9},{9,10},{10,1... | collective-permute-start | bytes 18824 | tf_op jit(solution)/shard_map/ppermute | solution.py:16
  12.1 9.1 %collective-permute-start.3 = (f32[2,8,98,1]{2,1,3,0:T(8,128)}, f32[2,8,98,1]{2,1,3,0:T(8,128)}, u32[]{:S(2)}, u32[]{:S(2)}) collective-permute-start(f32[2,8,98,1]{2,1,3,0:T(8,128)} %copy.49), channel_id=1, source_target_pairs={{1,0},{2,1},{3,2},{4,3},{5,4},{6,5},{7,6},{0,7},{9,8},{10,9},{11,1... | collective-permute-start | bytes 18824 | tf_op jit(solution)/shard_map/ppermute | solution.py:18
  19.2 4.0 %copy-start.4 = (f32[2,8,1,256]{3,1,2,0:T(8,128)S(1)}, f32[2,8,1,256]{3,1,2,0:T(8,128)}, u32[]{:S(2)}) copy-start(f32[2,8,1,256]{3,1,2,0:T(8,128)} %copy-done.3) | copy-start | bytes 49156
  19.2 4.0 %copy-start.6 = (f32[2,8,1,256]{3,1,2,0:T(8,128)S(1)}, f32[2,8,1,256]{3,1,2,0:T(8,128)}, u32[]{:S(2)}) copy-start(f32[2,8,1,256]{3,1,2,0:T(8,128)} %copy-done.5) | copy-start | bytes 49156
  19.2 3.9 %copy-start.8 = (f32[98]{0:T(128)S(1)}, f32[98]{0:T(128)}, u32[]{:S(2)}) copy-start(f32[98]{0:T(128)} %and_convert_fusion) | copy-start | bytes 1180
  23.2 2.4 %copy-start.7 = (f32[8]{0:T(128)S(1)}, f32[8]{0:T(128)}, u32[]{:S(2)}) copy-start(f32[8]{0:T(128)} %param.16) | copy-start | bytes 100
  27.8 3.8 %collective-permute-start.4 = (f32[2,8,1,256]{3,1,2,0:T(8,128)S(1)}, f32[2,8,1,256]{3,1,2,0:T(8,128)S(1)}, u32[]{:S(2)}, u32[]{:S(2)}) collective-permute-start(f32[2,8,1,256]{3,1,2,0:T(8,128)S(1)} %get-tuple-element.111), channel_id=1, source_target_pairs={{0,8},{8,0},{1,9},{9,1},{2,10},{10,2},{3,11},{11,3},{4,12},{12,4},... | collective-permute-start | bytes 49160 | tf_op jit(solution)/shard_map/ppermute | solution.py:16
  28.5 3.7 %collective-permute-start.5 = (f32[2,8,1,256]{3,1,2,0:T(8,128)S(1)}, f32[2,8,1,256]{3,1,2,0:T(8,128)S(1)}, u32[]{:S(2)}, u32[]{:S(2)}) collective-permute-start(f32[2,8,1,256]{3,1,2,0:T(8,128)S(1)} %get-tuple-element.112), channel_id=1, source_target_pairs={{8,0},{0,8},{9,1},{1,9},{10,2},{2,10},{11,3},{3,11},{12,4},{4,12},... | collective-permute-start | bytes 49160 | tf_op jit(solution)/shard_map/ppermute | solution.py:18
  35.2 5.2 %collective-permute-start.6 = (f32[2,8,98,1]{2,1,3,0:T(8,128)S(1)}, f32[2,8,98,1]{2,1,3,0:T(8,128)S(1)}, u32[]{:S(2)}, u32[]{:S(2)}) collective-permute-start(f32[2,8,98,1]{2,1,3,0:T(8,128)S(1)} %copy.54), channel_id=1, source_target_pairs={{0,1},{1,2},{2,3},{3,4},{4,5},{5,6},{6,7},{7,0},{8,9},{9,10},{10,1... | collective-permute-start | bytes 18824 | tf_op jit(solution)/shard_map/ppermute | solution.py:16
  36.7 5.1 %collective-permute-start.7 = (f32[2,8,98,1]{2,1,3,0:T(8,128)S(1)}, f32[2,8,98,1]{2,1,3,0:T(8,128)S(1)}, u32[]{:S(2)}, u32[]{:S(2)}) collective-permute-start(f32[2,8,98,1]{2,1,3,0:T(8,128)S(1)} %copy.55), channel_id=1, source_target_pairs={{1,0},{2,1},{3,2},{4,3},{5,4},{6,5},{7,6},{0,7},{9,8},{10,9},{11,1... | collective-permute-start | bytes 18824 | tf_op jit(solution)/shard_map/ppermute | solution.py:18
  48.7 6.2 %copy-start.10 = (s32[64]{0:T(128)S(1)}, s32[64]{0:T(128)}, u32[]{:S(2)}) copy-start(s32[64]{0:T(128)} %param.21) | copy-start | bytes 772
  49.9 17.8 %copy-start.11 = (s32[14]{0:T(128)S(1)}, s32[14]{0:T(128)}, u32[]{:S(2)}) copy-start(s32[14]{0:T(128)} %param.20) | copy-start | bytes 172
  49.9 17.4 %all-to-all-start = ((bf16[3,8,32,256]{3,1,0,2:T(8,128)(2,1)}), bf16[3,8,32,256]{3,1,0,2:T(8,128)(2,1)S(1)}, u32[]{:S(2)}, u32[]{:S(2)}) async-start(bf16[3,8,32,256]{3,1,0,2:T(8,128)(2,1)} %bitcast.13), calls=%async_computation | async-start | bytes 786432 | tf_op jit(solution)/shard_map/all_to_all | solution.py:128
where the time goes:
time: 162 us; the launch traced here: 159 us
  blocking collectives  38 us (23%)
  local copies, waits for them, and re-layouts  28.7 us (18%)
  loops' own time  27.6 us (17%)
  starting transfers between devices  17.5 us (11%)
  matrix products  16.7 us (10%)
  waiting for transfers between devices  15.2 us (9%)
  other arithmetic  14.2 us (9%)
    psum x1, blocking collectives, body(): numer = lax.psum(partial_value, ('role', 'gy', 'gx'))  38 us
    another operation x1, loops' own time, lon_remap(): result = lax.fori_loop(0, block_count, one_block, empty)  27.6 us
    dot_general x14, matrix products, one_block(): product = jnp.dot(window, weights, preferred_element_type=jnp.float32)  16 us
    all_to_all x1, waiting for transfers between devices, body(): lax.all_to_all(lat_out, 'gx', split_axis=2, concat_axis=3, tiled=True)  10.8 us
    ppermute x4, starting transfers between devices, with_halo(): lax.ppermute(head, axis, [((i + 1) % count, i) for i in range(count)])  8.75 us
    dynamic_slice x14, local copies, waits for them, and re-layouts, one_block(): start = panel_starting_source_meridian[index]  8.21 us
    all_to_all x1, starting transfers between devices, body(): lax.all_to_all(lat_out, 'gx', split_axis=2, concat_axis=3, tiled=True)  4.92 us
    mul x2, other arithmetic, clear_outside(): return padded * inside.astype(padded.dtype)  4.79 us
  transfers between devices with their start and end apart: 9, of which 5 were waited for; matrix products, arithmetic and copies ran while one was open for 7% of the time, Pallas kernels for 0%

commit v1 on v0

v1 whole, which is shorter than its diff:
```python
import functools
import math

import jax
import jax.numpy as jnp
import numpy as np
from jax import lax
from jax.experimental import pallas as pl
from jax.experimental.pallas import tpu as pltpu
from jax.sharding import PartitionSpec as P

LANES = 128
F32 = jnp.float32
BF16 = jnp.bfloat16
MESH = pl.DeviceIdType.MESH


def wrap(value, count):
    return jnp.where(value >= count, value - count, value)


def iota(shape, dim):
    return lax.broadcasted_iota(jnp.int32, shape, dim)


def peer_of(dims, d):
    n_role, n_gy, n_gx = dims[:3]
    role, gy, gx = (lax.axis_index(a) for a in ("role", "gy", "gx"))
    dx, dyr = d % n_gx, d // n_gx
    dy, dr = dyr % n_gy, dyr // n_gy
    return (wrap(role + dr, n_role), wrap(gy + dy, n_gy), wrap(gx + dx, n_gx))


def model_kernel(
    dims,
    temp_hbm,
    salt_hbm,
    zonal_hbm,
    merid_hbm,
    kappa_ref,
    land_ref,
    band_ref,
    lat_out,
    x0,
    x1,
    zonal,
    merid,
    band_rows,
    means,
    lat_send,
    lat_recv,
    row_send,
    row_recv,
    col_send,
    col_recv,
    in_sems,
    halo_send_sems,
    halo_recv_sems,
    a2a_send_sems,
    a2a_recv_sems,
    local_sems,
):
    n_role, n_gy, n_gx, levels, cy, cx, trows, srows, nblk, sw, tb, groups = dims
    role, gy, gx = (lax.axis_index(a) for a in ("role", "gy", "gx"))
    lev_grp = 16 // trows
    halves = levels // lev_grp

    loads = [
        pltpu.make_async_copy(temp_hbm, x0.at[0], in_sems.at[0]),
        pltpu.make_async_copy(salt_hbm, x0.at[1], in_sems.at[1]),
        pltpu.make_async_copy(zonal_hbm, zonal, in_sems.at[2]),
        pltpu.make_async_copy(merid_hbm, merid, in_sems.at[3]),
    ]
    for load in loads:
        load.start()

    peer = functools.partial(peer_of, dims)
    barrier = pltpu.get_barrier_semaphore()
    greeted = [d for d in range(1, n_gx)] + [d * n_gx for d in range(1, n_role * n_gy)]
    for d in greeted:
        pl.semaphore_signal(barrier, inc=1, device_id=peer(d), device_id_type=MESH)

    band_rows[...] = jnp.zeros_like(band_rows)

    lane = iota((cy, LANES), 1)

    def pack_columns(s, tiles):
        first = jnp.zeros((cy, LANES), F32)
        last = jnp.zeros((cy, LANES), F32)
        for t in range(2):
            for l in range(levels):
                k = t * levels + l
                head = tiles[t, l, :, pl.ds(0, LANES)]
                tail = tiles[t, l, :, pl.ds(cx - LANES, LANES)]
                first = jnp.where(lane == k, pltpu.roll(head, k, 1) if k else head, first)
                last = jnp.where(lane == k, pltpu.roll(tail, k + 1, 1), last)
        col_send[s, 0] = first
        col_send[s, 1] = last

    def pack_rows(s, t, l, head, tail):
        row_send[s, 0, t, pl.ds(l, 1), :] = head
        row_send[s, 1, t, pl.ds(l, 1), :] = tail

    west = wrap(gx + n_gx - 1, n_gx)
    east = wrap(gx + 1, n_gx)
    below = wrap(gy + n_gy - 1, n_gy)
    above = wrap(gy + 1, n_gy)

    def halo_copies(s):
        copies = []
        for i, (send, recv, d, target) in enumerate(
            (
                (col_send, col_recv, 0, (role, gy, west)),
                (col_send, col_recv, 1, (role, gy, east)),
                (row_send, row_recv, 0, (role, below, gx)),
                (row_send, row_recv, 1, (role, above, gx)),
            )
        ):
            copies.append(
                pltpu.make_async_remote_copy(
                    src_ref=send.at[s, d],
                    dst_ref=recv.at[s, d],
                    send_sem=halo_send_sems.at[s, i],
                    recv_sem=halo_recv_sems.at[s, i],
                    device_id=target,
                    device_id_type=MESH,
                )
            )
        return copies

    loads[0].wait()
    loads[1].wait()
    for t in range(2):
        for l in range(levels):
            pack_rows(0, t, l, x0[t, l, pl.ds(0, 1), :], x0[t, l, pl.ds(cy - 1, 1), :])
    pack_columns(0, x0)
    pl.semaphore_wait(barrier, len(greeted))
    halo0 = halo_copies(0)
    for copy in halo0:
        copy.start()

    for g in range(n_gx):
        band_rows[pl.ds(g * trows, trows), pl.ds(0, srows)] = band_ref[g].astype(F32)
    brows = band_rows.shape[0]
    out_r, in_r = n_gx * lev_grp * trows, lev_grp * cy
    ri, rq = iota((out_r, brows), 0), iota((out_r, brows), 1)
    pick_r = (lax.div(ri, lev_grp * trows) == lax.div(rq, trows)) & (
        lax.rem(ri, trows) == lax.rem(rq, trows)
    )
    spread = jnp.dot(
        pick_r.astype(F32).astype(BF16), band_rows[...].astype(BF16), preferred_element_type=F32
    )
    cs, cc = iota((LANES, in_r), 0), iota((LANES, in_r), 1)
    pick_c = lax.rem(lax.rem(cc, cy), srows) == cs
    spread = jnp.dot(
        spread.astype(BF16), pick_c.astype(F32).astype(BF16), preferred_element_type=F32
    )
    ai, ac = iota((out_r, in_r), 0), iota((out_r, in_r), 1)
    keep = (lax.div(lax.rem(ai, lev_grp * trows), trows) == lax.div(ac, cy)) & (
        lax.div(lax.rem(ac, cy), srows) == lax.div(ai, lev_grp * trows)
    )
    band = jnp.where(keep, spread, 0.0).astype(BF16)

    number = gy * n_gx + gx
    ocean = jnp.ones((1, cx), F32)
    for i in range(land_ref.shape[0]):
        ocean = jnp.where(jnp.full((1, cx), land_ref[i], jnp.int32) == number, 0.0, ocean)

    wide = iota((cy, cx), 1)
    tall = iota((cy, cx), 0)
    has_above = jnp.where(gy < n_gy - 1, 1.0, 0.0).astype(F32)
    has_below = jnp.where(gy > 0, 1.0, 0.0).astype(F32)

    def advance(s, tiles, l):
        u = zonal[l].astype(F32) * (0.5 * ocean)
        v = merid[l].astype(F32) * (0.5 * ocean)
        kap = kappa_ref[l] * ocean
        own = 1.0 - 4.0 * kap
        results = []
        for t in range(2):
            k = t * levels + l
            c = tiles[t, l]
            e = jnp.where(
                wide == cx - 1, col_recv[s, 0, :, pl.ds(k, 1)], pltpu.roll(c, cx - 1, 1)
            )
            w = jnp.where(wide == 0, col_recv[s, 1, :, pl.ds(k, 1)], pltpu.roll(c, 1, 1))
            n = jnp.where(
                tall == cy - 1,
                row_recv[s, 0, t, pl.ds(l, 1), :] * has_above,
                pltpu.roll(c, cy - 1, 0),
            )
            b = jnp.where(
                tall == 0, row_recv[s, 1, t, pl.ds(l, 1), :] * has_below, pltpu.roll(c, 1, 0)
            )
            results.append(
                own * c + (kap * (e + w + n + b) - u * (e - w) - v * (n - b))
            )
        return results

    loads[2].wait()
    loads[3].wait()
    for copy in halo0:
        copy.wait()
    for l in range(levels):
        new = advance(0, x0, l)
        for t in range(2):
            x1[t, l] = new[t]
            pack_rows(1, t, l, new[t][:1], new[t][cy - 1 :])
    pack_columns(1, x1)
    halo1 = halo_copies(1)
    for copy in halo1:
        copy.start()

    for copy in halo1:
        copy.wait()

    mine = pl.multiple_of(gx * cx, LANES)
    exchanges = []
    local = []
    for h in range(halves):
        for l in range(h * lev_grp, (h + 1) * lev_grp):
            new = advance(1, x1, l)
            lev = (role * levels + l).astype(F32)
            factor = 0.17 * (1.0 + 0.03 * lev)
            t1, s1 = x1[0, l], x1[1, l]
            t2, s2 = new
            r1 = 0.78 * s1 - factor * t1 - 0.02 * t1 * t1
            r2 = 0.78 * s2 - factor * t2 - 0.02 * t2 * t2
            means[0, l] = (0.5 * (t1 + t2)).astype(BF16)
            means[1, l] = (0.5 * (s1 + s2)).astype(BF16)
            means[2, l] = (0.5 * (r1 + r2)).astype(BF16)
        for f in range(3):
            rows = means[f, pl.ds(h * lev_grp, lev_grp)].reshape(in_r, cx)
            lat = jnp.dot(band, rows, preferred_element_type=F32).astype(BF16)
            for g in range(n_gx):
                lat_send[g, f, h] = lat[g * 16 : (g + 1) * 16]
        for d in range(1, n_gx):
            target = wrap(gx + d, n_gx)
            copy = pltpu.make_async_remote_copy(
                src_ref=lat_send.at[target, :, h],
                dst_ref=lat_recv.at[:, h, :, pl.ds(mine, cx)],
                send_sem=a2a_send_sems.at[h, d],
                recv_sem=a2a_recv_sems.at[h, d],
                device_id=(role, gy, target),
                device_id_type=MESH,
            )
            copy.start()
            exchanges.append((h, copy))
        copy = pltpu.make_async_copy(
            lat_send.at[gx, :, h], lat_recv.at[:, h, :, pl.ds(mine, cx)], local_sems.at[h]
        )
        copy.start()
        local.append(copy)

    for _, copy in exchanges:
        copy.wait()
    for copy in local:
        copy.wait()
    lat_out[:, :, :, pl.ds(0, n_gx * cx)] = lat_recv[...]
    lat_out[:, :, :, pl.ds(n_gx * cx, LANES)] = jnp.zeros(lat_out.shape[:3] + (LANES,), BF16)


def remap_kernel(
    dims, lat_ref, panel_hbm, start_ref, cluster_ref, area_ref, out_ref, part_ref, panel, pad, sems
):
    n_role, n_gy, n_gx, levels, cy, cx, trows, srows, nblk, sw, tb, groups = dims
    role, gy, gx = (lax.axis_index(a) for a in ("role", "gy", "gx"))
    loads = [
        pltpu.make_async_copy(panel_hbm.at[j], panel.at[j], sems.at[j]) for j in range(nblk)
    ]
    for load in loads:
        load.start()
    pad[:, pl.ds(0, LANES), :] = jnp.zeros((nblk, LANES, tb), F32)
    pad[:, pl.ds(LANES + sw, LANES), :] = jnp.zeros((nblk, LANES, tb), F32)

    glanes = part_ref.shape[1]
    labels = iota((1, glanes), 1)

    def add_area(r, so_far):
        return so_far + jnp.where(labels == cluster_ref[r], area_ref[r], 0.0)

    zero = jnp.zeros((1, glanes), F32)
    all_rows = cluster_ref.shape[0]
    area_sum = lax.fori_loop(0, all_rows, add_area, zero, unroll=8)
    thick_total = sum(1.0 + 0.25 * k for k in range(levels * n_role))
    denom = area_sum * (thick_total * nblk * tb)

    first_row = (gy * n_gx + gx) * trows
    out_rows = 3 * levels * trows
    row = iota((out_rows, 1), 0)
    ti = lax.rem(row, trows)
    hot = jnp.zeros((out_rows, glanes), F32)
    for t in range(trows):
        row_hot = jnp.where(labels == cluster_ref[first_row + t], area_ref[first_row + t], 0.0)
        hot = jnp.where(ti == t, row_hot, hot)
    level = role * levels + lax.rem(lax.div(row, trows), levels)
    thick = 1.0 + 0.25 * level.astype(F32)

    squares = jnp.zeros((out_rows, tb), F32)
    for j in range(nblk):
        start = start_ref[j]
        base = lax.div(start, LANES) * LANES
        loads[j].wait()
        pad[j, pl.ds(LANES, sw), :] = panel[j].astype(F32)
        weights = pad[j, pl.ds(LANES - (start - base), sw + LANES), :].astype(BF16)
        window = lat_ref[:, pl.ds(pl.multiple_of(base, LANES), sw + LANES)]
        values = jnp.dot(window, weights, preferred_element_type=F32)
        squares = squares + values * values
        out_ref[:, pl.ds(j * tb, tb)] = values.astype(BF16)
    weighted = jnp.sum(squares, axis=1, keepdims=True) * thick * hot
    part_ref[...] = jnp.zeros_like(part_ref)
    named = labels < groups
    for f in range(3):
        size = levels * trows
        numer = jnp.sum(weighted[f * size : (f + 1) * size], axis=0, keepdims=True)
        part_ref[pl.ds(f, 1), :] = jnp.where(named, numer / jnp.where(named, denom, 1.0), 0.0)


def sums_kernel(dims, part_ref, sums_ref, gather, sum_sems):
    n_role, n_gy, n_gx = dims[:3]
    groups = dims[-1]
    role, gy, gx = (lax.axis_index(a) for a in ("role", "gy", "gx"))
    total = n_role * n_gy * n_gx
    me = (role * n_gy + gy) * n_gx + gx
    barrier = pltpu.get_barrier_semaphore()

    def for_others(do):
        if total <= 64:
            for d in range(1, total):
                do(peer_of(dims, d))
        else:

            @pl.loop(1, total)
            def _(d):
                do(peer_of(dims, d))

    def greet(device):
        pl.semaphore_signal(barrier, inc=1, device_id=device, device_id_type=MESH)

    def send(device):
        pltpu.make_async_remote_copy(
            src_ref=gather.at[me],
            dst_ref=gather.at[me],
            send_sem=sum_sems.at[0],
            recv_sem=sum_sems.at[1],
            device_id=device,
            device_id_type=MESH,
        ).start()

    for_others(greet)
    gather[me] = part_ref[...]
    pl.semaphore_wait(barrier, total - 1)
    for_others(send)
    every = gather.at[pl.ds(0, total - 1)]
    for i in (1, 0):
        pltpu.make_async_copy(every, every, sum_sems.at[i]).wait()
    sums_ref[...] = jnp.sum(gather[...], axis=0)[:3, :groups]


def body(
    dims,
    area,
    thermal_anomaly,
    saltiness_anomaly,
    zonal_flow_fraction,
    meridional_flow_fraction,
    mixing_coefficient,
    continent_patch_numbering,
    parallel_band_coefficients,
    meridian_panel_coefficients,
    panel_starting_source_meridian,
    target_parallel_cluster,
):
    n_role, n_gy, n_gx, levels, cy, cx, trows, srows, nblk, sw, tb, groups = dims
    total = n_role * n_gy * n_gx
    lev_grp = 16 // trows
    halves = levels // lev_grp
    glanes = -(-groups // LANES) * LANES
    hbm = pl.BlockSpec(memory_space=pl.ANY)
    smem = pl.BlockSpec(memory_space=pltpu.SMEM)
    vmem = pl.BlockSpec(memory_space=pltpu.VMEM)
    brows = -(-n_gx * trows // LANES) * LANES
    dma = pltpu.SemaphoreType.DMA
    mib = 1024 * 1024
    lat = pl.pallas_call(
        functools.partial(model_kernel, dims),
        out_shape=jax.ShapeDtypeStruct((3, halves, 16, n_gx * cx + LANES), BF16),
        in_specs=[hbm] * 4 + [smem, smem, vmem],
        out_specs=vmem,
        scratch_shapes=[
            pltpu.VMEM((2, levels, cy, cx), F32),
            pltpu.VMEM((2, levels, cy, cx), F32),
            pltpu.VMEM((levels, cy, cx), BF16),
            pltpu.VMEM((levels, cy, cx), BF16),
            pltpu.VMEM((brows, LANES), F32),
            pltpu.VMEM((3, levels, cy, cx), BF16),
            pltpu.VMEM((n_gx, 3, halves, 16, cx), BF16),
            pltpu.VMEM((3, halves, 16, n_gx * cx), BF16),
            pltpu.VMEM((2, 2, 2, levels, cx), F32),
            pltpu.VMEM((2, 2, 2, levels, cx), F32),
            pltpu.VMEM((2, 2, cy, LANES), F32),
            pltpu.VMEM((2, 2, cy, LANES), F32),
            dma((4,)),
            dma((2, 4)),
            dma((2, 4)),
            dma((halves, n_gx)),
            dma((halves, n_gx)),
            dma((halves,)),
        ],
        compiler_params=pltpu.CompilerParams(
            collective_id=0, has_side_effects=True, vmem_limit_bytes=20 * mib
        ),
        name="model",
    )(
        thermal_anomaly,
        saltiness_anomaly,
        zonal_flow_fraction,
        meridional_flow_fraction,
        mixing_coefficient,
        continent_patch_numbering,
        parallel_band_coefficients,
    )
    out_rows = 3 * levels * trows
    remapped, part = pl.pallas_call(
        functools.partial(remap_kernel, dims),
        out_shape=(
            jax.ShapeDtypeStruct((out_rows, nblk * tb), BF16),
            jax.ShapeDtypeStruct((8, glanes), F32),
        ),
        in_specs=[vmem, hbm, smem, smem, smem],
        out_specs=(vmem, vmem),
        scratch_shapes=[
            pltpu.VMEM((nblk, sw, tb), BF16),
            pltpu.VMEM((nblk, sw + 2 * LANES, tb), F32),
            dma((nblk,)),
        ],
        compiler_params=pltpu.CompilerParams(vmem_limit_bytes=30 * mib),
        name="remap",
    )(
        lat.reshape(out_rows, n_gx * cx + LANES),
        meridian_panel_coefficients,
        panel_starting_source_meridian,
        target_parallel_cluster,
        jnp.asarray(area),
    )
    sums = pl.pallas_call(
        functools.partial(sums_kernel, dims),
        out_shape=jax.ShapeDtypeStruct((3, groups), F32),
        in_specs=[vmem],
        out_specs=vmem,
        scratch_shapes=[pltpu.VMEM((total, 8, glanes), F32), dma((2,))],
        compiler_params=pltpu.CompilerParams(
            collective_id=1, has_side_effects=True, vmem_limit_bytes=16 * mib
        ),
        name="sums",
    )(part)
    return remapped.reshape(3, levels, trows, nblk * tb), sums


def solution(mesh):
    in_specs = (
        P("role", "gy", "gx"),
        P("role", "gy", "gx"),
        P("role", "gy", "gx"),
        P("role", "gy", "gx"),
        P("role"),
        P(),
        P("gy", None, None),
        P(),
        P(),
        P(),
    )
    out_specs = (P(None, "role", ("gy", "gx"), None), P())

    def run(*args):
        n_role, n_gy, n_gx = (mesh.shape[a] for a in ("role", "gy", "gx"))
        levels, rows, cols = args[0].shape
        _, trows, srows = args[6].shape
        nblk, sw, tb = args[7].shape
        dims = (
            n_role,
            n_gy,
            n_gx,
            levels // n_role,
            rows // n_gy,
            cols // n_gx,
            trows,
            srows,
            nblk,
            sw,
            tb,
            4 * n_gy,
        )
        nrows = args[9].shape[0]
        r = np.arange(nrows, dtype=np.float64)
        area = np.cos((-75.0 + 150.0 * (r + 0.5) / nrows) * (math.pi / 180.0)).astype(np.float32)
        return jax.shard_map(
            functools.partial(body, dims, area),
            mesh=mesh,
            in_specs=in_specs,
            out_specs=out_specs,
            check_vma=False,
        )(*args)

    return run
```

time: 162 us -> 49.3 us (0.30); the launches traced: 159 us -> 49 us
  Pallas kernels: 0 us -> 40.5 us
  blocking collectives: 38 us -> 0 us
  loops' own time: 27.6 us -> 0 us
  local copies, waits for them, and re-layouts: 28.7 us -> 7.8 us
  starting transfers between devices: 17.5 us -> 0 us
  matrix products: 16.7 us -> 0 us
  waiting for transfers between devices: 15.2 us -> 0 us
  other arithmetic: 14.2 us -> 0 us
    pallas_call x0 -> x3, Pallas kernels: none -> 40.5 us  [the longest x1 25.4 us: body(): pl.pallas_call(functools.partial(model_kernel, dims), out_shape=jax.Shape...]
    psum x1 -> x0, blocking collectives: 38 us -> none  [body(): numer = lax.psum(partial_value, ('role', 'gy', 'gx'))]
    another operation x1 -> x0, loops' own time: 27.6 us -> none  [lon_remap(): result = lax.fori_loop(0, block_count, one_block, empty)]
    dot_general x17 -> x0, matrix products: 16.7 us -> none  [the longest x14 16 us: one_block(): product = jnp.dot(window, weights, preferred_element_type=jnp.float32)]
    ppermute x8 -> x0, starting transfers between devices: 12.6 us -> none  [the longest x4 8.75 us: with_halo(): lax.ppermute(head, axis, [((i + 1) % count, i) for i in range(count)])]
    all_to_all x1 -> x0, waiting for transfers between devices: 10.8 us -> none  [body(): lax.all_to_all(lat_out, 'gx', split_axis=2, concat_axis=3, tiled=True)]
    dynamic_slice x16 -> x0, local copies, waits for them, and re-layouts: 8.36 us -> none  [the longest x14 8.21 us: one_block(): start = panel_starting_source_meridian[index]]
    slice x8 -> x0, local copies, waits for them, and re-layouts: 7.01 us -> none  [the longest x5 3.43 us: with_halo(): lax.slice_in_dim(cells, cells.shape[dim] - width, cells.shape[dim], axis=...]
  transfers between devices with their start and end apart: 9 -> 0, of which waited for: 5 -> 0; matrix products, arithmetic and copies ran while one was open for 7% -> 0% of each run, Pallas kernels for 0% -> 0%
where the time goes in v1:
time: 49.3 us; the launch traced here: 49 us
  Pallas kernels  40.5 us (82%)
  local copies, waits for them, and re-layouts  7.8 us (16%)
  between operations  0.71 us (1%)
    pallas_call x1, Pallas kernels, body(): pl.pallas_call(functools.partial(model_kernel, dims), out_shape=jax.Shape...  25.4 us
    pallas_call x1, Pallas kernels, body(): pl.pallas_call(functools.partial(sums_kernel, dims), out_shape=jax.ShapeD...  8.78 us
    unnamed x23, local copies, waits for them, and re-layouts  6.98 us
    pallas_call x1, Pallas kernels, body(): pl.pallas_call(functools.partial(remap_kernel, dims), out_shape=(jax.Shap...  6.29 us

profile of v1, /device:TPU:0, one launch (start us, length us, event | category | flops | bytes accessed | tf_op | source)
XLA Modules:
  0.0 49.0 jit_solution(17532064549602244408)
XLA Ops:
  0.6 0.0 copy-start
  0.6 0.0 copy-start.1
  0.7 1.3 %copy-done.1 = f32[8,96,256]{2,1,0:T(8,128)S(1)} copy-done((f32[8,96,256]{2,1,0:T(8,128)S(1)}, f32[8,96,256]{2,1,0:T(8,128)}, u32[]{:S(2)}) %copy-start.1) | copy-done | bytes 786456
  1.9 0.0 copy-start.2
  1.9 1.1 %copy-done.2 = f32[8,96,256]{2,1,0:T(8,128)S(1)} copy-done((f32[8,96,256]{2,1,0:T(8,128)S(1)}, f32[8,96,256]{2,1,0:T(8,128)}, u32[]{:S(2)}) %copy-start.2) | copy-done | bytes 786456
  3.0 0.0 copy-start.3
  3.0 1.0 %copy-done.3 = bf16[8,96,256]{2,1,0:T(8,128)(2,1)S(1)} copy-done((bf16[8,96,256]{2,1,0:T(8,128)(2,1)S(1)}, bf16[8,96,256]{2,1,0:T(8,128)(2,1)}, u32[]{:S(2)}) %copy-start.3) | copy-done | bytes 393240
  4.0 0.0 copy-start.4
  4.0 1.0 %copy-done.4 = bf16[8,96,256]{2,1,0:T(8,128)(2,1)S(1)} copy-done((bf16[8,96,256]{2,1,0:T(8,128)(2,1)S(1)}, bf16[8,96,256]{2,1,0:T(8,128)(2,1)}, u32[]{:S(2)}) %copy-start.4) | copy-done | bytes 393240
  5.0 0.0 copy-start.5
  5.0 0.7 %copy-done.5 = bf16[8,4,12]{2,1,0:T(4,128)(2,1)S(1)} copy-done((bf16[8,4,12]{2,1,0:T(4,128)(2,1)S(1)}, bf16[8,4,12]{2,1,0:T(4,128)(2,1)}, u32[]{:S(2)}) %copy-start.5) | copy-done | bytes 792
  5.7 0.0 copy-start.6
  5.7 0.7 %copy-done.6 = f32[8]{0:T(128)S(1)} copy-done((f32[8]{0:T(128)S(1)}, f32[8]{0:T(128)}, u32[]{:S(2)}) %copy-start.6) | copy-done | bytes 56
  6.4 0.0 copy-start.7
  6.4 0.7 %copy-done.7 = s32[2]{0:T(128)S(1)} copy-done((s32[2]{0:T(128)S(1)}, s32[2]{0:T(128)}, u32[]{:S(2)}) %copy-start.7) | copy-done | bytes 32
  7.1 25.4 %model.1 = bf16[3,2,16,2176]{3,2,1,0:T(8,128)(2,1)S(1)} custom-call(f32[8,96,256]{2,1,0:T(8,128)S(1)} %copy-done.1, f32[8,96,256]{2,1,0:T(8,128)S(1)} %copy-done.2, bf16[8,96,256]{2,1,0:T(8,128)(2,1)S(1)} %copy-done.3, bf16[8,96,256]{2,1,0:T(8,128)(2,1)S(1)} %copy-done.4, f32[8]{0:T(128)S(1)} %copy-done.6, s32[2]{0:T(128)S(1)} %copy-done.7, ...), custom_call_target="tpu_custom_call" | custom-call | tf_op jit(solution)/shard_map/model/pallas_call | solution.py:385
  32.5 0.0 copy-done
  32.5 0.0 copy-done.8
  32.5 0.0 copy-done.9
  32.5 0.0 copy-done.10
  32.5 6.3 %remap.1 = (bf16[96,1792]{1,0:T(8,128)(2,1)S(1)}, f32[8,128]{1,0:T(8,128)S(1)}) custom-call(bf16[96,2176]{1,0:T(8,128)(2,1)S(1)} %bitcast.1, bf16[14,512,128]{2,1,0:T(8,128)(2,1)S(1)} %copy-done, s32[14]{0:T(128)S(1)} %copy-done.8, s32[64]{0:T(128)S(1)} %copy-done.9, f32[64]{0:T(128)S(1)} %copy-done.10), custom_call_target="tpu_custom_call" | custom-call | tf_op jit(solution)/shard_map/remap/pallas_call | solution.py:424
  38.8 0.8 %reshape.11 = bf16[3,8,4,1792]{3,2,1,0:T(4,128)(2,1)} reshape(bf16[96,1792]{1,0:T(8,128)(2,1)S(1)} %get-tuple-element.4) | data formatting | bytes 688128 | tf_op jit(solution)/shard_map/reshape | solution.py:457
  39.6 8.8 %sums.1 = f32[3,8]{1,0:T(4,128)S(1)} custom-call(f32[8,128]{1,0:T(8,128)S(1)} %get-tuple-element.5.part_ref), custom_call_target="tpu_custom_call" | custom-call | tf_op jit(solution)/shard_map/sums/pallas_call | solution.py:446
  48.4 0.6 %copy.14 = f32[3,8]{1,0:T(4,128)} copy(f32[3,8]{1,0:T(4,128)S(1)} %sums.1) | data formatting | bytes 192
  (3 shorter events, 0.0 us)
Async XLA Ops:
  0.6 31.8 %copy-start = (bf16[14,512,128]{2,1,0:T(8,128)(2,1)S(1)}, bf16[14,512,128]{2,1,0:T(8,128)(2,1)}, u32[]{:S(2)}) copy-start(bf16[14,512,128]{2,1,0:T(8,128)(2,1)} %panel_hbm.1) | copy-start | bytes 5505028
  0.6 1.3 %copy-start.1 = (f32[8,96,256]{2,1,0:T(8,128)S(1)}, f32[8,96,256]{2,1,0:T(8,128)}, u32[]{:S(2)}) copy-start(f32[8,96,256]{2,1,0:T(8,128)} %temp_hbm.1) | copy-start | bytes 2359300
  1.9 1.1 %copy-start.2 = (f32[8,96,256]{2,1,0:T(8,128)S(1)}, f32[8,96,256]{2,1,0:T(8,128)}, u32[]{:S(2)}) copy-start(f32[8,96,256]{2,1,0:T(8,128)} %salt_hbm.1) | copy-start | bytes 2359300
  3.0 1.0 %copy-start.3 = (bf16[8,96,256]{2,1,0:T(8,128)(2,1)S(1)}, bf16[8,96,256]{2,1,0:T(8,128)(2,1)}, u32[]{:S(2)}) copy-start(bf16[8,96,256]{2,1,0:T(8,128)(2,1)} %zonal_hbm.1) | copy-start | bytes 1179652
  4.0 1.0 %copy-start.4 = (bf16[8,96,256]{2,1,0:T(8,128)(2,1)S(1)}, bf16[8,96,256]{2,1,0:T(8,128)(2,1)}, u32[]{:S(2)}) copy-start(bf16[8,96,256]{2,1,0:T(8,128)(2,1)} %merid_hbm.1) | copy-start | bytes 1179652
  5.0 0.7 %copy-start.5 = (bf16[8,4,12]{2,1,0:T(4,128)(2,1)S(1)}, bf16[8,4,12]{2,1,0:T(4,128)(2,1)}, u32[]{:S(2)}) copy-start(bf16[8,4,12]{2,1,0:T(4,128)(2,1)} %band_ref.1) | copy-start | bytes 2308
  5.7 0.7 %copy-start.6 = (f32[8]{0:T(128)S(1)}, f32[8]{0:T(128)}, u32[]{:S(2)}) copy-start(f32[8]{0:T(128)} %kappa_ref.1) | copy-start | bytes 100
  6.4 0.7 %copy-start.7 = (s32[2]{0:T(128)S(1)}, s32[2]{0:T(128)}, u32[]{:S(2)}) copy-start(s32[2]{0:T(128)} %land_ref.1) | copy-start | bytes 28
  7.0 25.4 %copy-start.8 = (s32[14]{0:T(128)S(1)}, s32[14]{0:T(128)}, u32[]{:S(2)}) copy-start(s32[14]{0:T(128)} %start_ref.1) | copy-start | bytes 172
  7.0 25.4 %copy-start.9 = (s32[64]{0:T(128)S(1)}, s32[64]{0:T(128)}, u32[]{:S(2)}) copy-start(s32[64]{0:T(128)} %cluster_ref.1) | copy-start | bytes 772
  7.0 25.4 %copy-start.10 = (f32[64]{0:T(128)S(1)}, f32[64]{0:T(128)}, u32[]{:S(2)}) copy-start(f32[64]{0:T(128)} %constant.2.clone.area_ref) | copy-start | bytes 772

commit v2 on v1

--- a/solution.py
+++ b/solution.py
@@ -59,6 +59,7 @@
     a2a_send_sems,
     a2a_recv_sems,
     local_sems,
+    out_sems,
 ):
     n_role, n_gy, n_gx, levels, cy, cx, trows, srows, nblk, sw, tb, groups = dims
     role, gy, gx = (lax.axis_index(a) for a in ("role", "gy", "gx"))
@@ -252,29 +253,48 @@
         copy.start()
         local.append(copy)
 
+    stores = []
+    for h in range(halves):
+        for when, copy in exchanges:
+            if when == h:
+                copy.wait_recv()
+        local[h].wait()
+        store = pltpu.make_async_copy(lat_recv.at[:, h], lat_out.at[:, h], out_sems.at[h])
+        store.start()
+        stores.append(store)
     for _, copy in exchanges:
-        copy.wait()
-    for copy in local:
-        copy.wait()
-    lat_out[:, :, :, pl.ds(0, n_gx * cx)] = lat_recv[...]
-    lat_out[:, :, :, pl.ds(n_gx * cx, LANES)] = jnp.zeros(lat_out.shape[:3] + (LANES,), BF16)
+        copy.wait_send()
+    for store in stores:
+        store.wait()
 
 
 def remap_kernel(
-    dims, lat_ref, panel_hbm, start_ref, cluster_ref, area_ref, out_ref, part_ref, panel, pad, sems
+    dims,
+    lat_hbm,
+    panel_hbm,
+    start_ref,
+    cluster_ref,
+    area_ref,
+    out_ref,
+    part_ref,
+    lat,
+    wide,
+    panel,
+    sems,
 ):
     n_role, n_gy, n_gx, levels, cy, cx, trows, srows, nblk, sw, tb, groups = dims
     role, gy, gx = (lax.axis_index(a) for a in ("role", "gy", "gx"))
+    lat_load = pltpu.make_async_copy(lat_hbm, lat, sems.at[nblk])
+    lat_load.start()
     loads = [
         pltpu.make_async_copy(panel_hbm.at[j], panel.at[j], sems.at[j]) for j in range(nblk)
     ]
     for load in loads:
         load.start()
-    pad[:, pl.ds(0, LANES), :] = jnp.zeros((nblk, LANES, tb), F32)
-    pad[:, pl.ds(LANES + sw, LANES), :] = jnp.zeros((nblk, LANES, tb), F32)
 
     glanes = part_ref.shape[1]
-    labels = iota((1, glanes), 1)
+    lanes = iota((1, glanes), 1)
+    labels = lax.rem(lanes, groups)
 
     def add_area(r, so_far):
         return so_far + jnp.where(labels == cluster_ref[r], area_ref[r], 0.0)
@@ -296,29 +316,43 @@
     level = role * levels + lax.rem(lax.div(row, trows), levels)
     thick = 1.0 + 0.25 * level.astype(F32)
 
+    lat_load.wait()
+    columns = n_gx * cx
+    wide[:, pl.ds(0, columns)] = lat[...].astype(F32)
+    wide[:, pl.ds(columns, LANES)] = jnp.zeros((out_rows, LANES), F32)
+    lane = iota((out_rows, LANES), 1)
     squares = jnp.zeros((out_rows, tb), F32)
     for j in range(nblk):
         start = start_ref[j]
         base = lax.div(start, LANES) * LANES
+        shift = LANES - (start - base)
+        turned = []
+        for i in range(sw // LANES + 1):
+            tile = wide[:, pl.ds(pl.multiple_of(base + i * LANES, LANES), LANES)]
+            turned.append(pltpu.roll(tile, lax.rem(shift, LANES), 1))
+        window = jnp.concatenate(
+            [
+                jnp.where(lane < shift, turned[i], turned[i + 1]).astype(BF16)
+                for i in range(sw // LANES)
+            ],
+            axis=1,
+        )
         loads[j].wait()
-        pad[j, pl.ds(LANES, sw), :] = panel[j].astype(F32)
-        weights = pad[j, pl.ds(LANES - (start - base), sw + LANES), :].astype(BF16)
-        window = lat_ref[:, pl.ds(pl.multiple_of(base, LANES), sw + LANES)]
-        values = jnp.dot(window, weights, preferred_element_type=F32)
+        values = jnp.dot(window, panel[j], preferred_element_type=F32)
         squares = squares + values * values
         out_ref[:, pl.ds(j * tb, tb)] = values.astype(BF16)
     weighted = jnp.sum(squares, axis=1, keepdims=True) * thick * hot
-    part_ref[...] = jnp.zeros_like(part_ref)
-    named = labels < groups
+    size = levels * trows
+    field = lax.div(lanes, groups)
+    numer = jnp.zeros((1, glanes), F32)
     for f in range(3):
-        size = levels * trows
-        numer = jnp.sum(weighted[f * size : (f + 1) * size], axis=0, keepdims=True)
-        part_ref[pl.ds(f, 1), :] = jnp.where(named, numer / jnp.where(named, denom, 1.0), 0.0)
+        own = jnp.sum(weighted[f * size : (f + 1) * size], axis=0, keepdims=True)
+        numer = jnp.where(field == f, own, numer)
+    part_ref[...] = numer / denom
 
 
 def sums_kernel(dims, part_ref, sums_ref, gather, sum_sems):
     n_role, n_gy, n_gx = dims[:3]
-    groups = dims[-1]
     role, gy, gx = (lax.axis_index(a) for a in ("role", "gy", "gx"))
     total = n_role * n_gy * n_gx
     me = (role * n_gy + gy) * n_gx + gx
@@ -354,7 +388,7 @@
     every = gather.at[pl.ds(0, total - 1)]
     for i in (1, 0):
         pltpu.make_async_copy(every, every, sum_sems.at[i]).wait()
-    sums_ref[...] = jnp.sum(gather[...], axis=0)[:3, :groups]
+    sums_ref[...] = jnp.sum(gather[...], axis=0)
 
 
 def body(
@@ -375,7 +409,7 @@
     total = n_role * n_gy * n_gx
     lev_grp = 16 // trows
     halves = levels // lev_grp
-    glanes = -(-groups // LANES) * LANES
+    glanes = -(-3 * groups // LANES) * LANES
     hbm = pl.BlockSpec(memory_space=pl.ANY)
     smem = pl.BlockSpec(memory_space=pltpu.SMEM)
     vmem = pl.BlockSpec(memory_space=pltpu.VMEM)
@@ -384,9 +418,9 @@
     mib = 1024 * 1024
     lat = pl.pallas_call(
         functools.partial(model_kernel, dims),
-        out_shape=jax.ShapeDtypeStruct((3, halves, 16, n_gx * cx + LANES), BF16),
+        out_shape=jax.ShapeDtypeStruct((3, halves, 16, n_gx * cx), BF16),
         in_specs=[hbm] * 4 + [smem, smem, vmem],
-        out_specs=vmem,
+        out_specs=hbm,
         scratch_shapes=[
             pltpu.VMEM((2, levels, cy, cx), F32),
             pltpu.VMEM((2, levels, cy, cx), F32),
@@ -406,9 +440,10 @@
             dma((halves, n_gx)),
             dma((halves, n_gx)),
             dma((halves,)),
+            dma((halves,)),
         ],
         compiler_params=pltpu.CompilerParams(
-            collective_id=0, has_side_effects=True, vmem_limit_bytes=20 * mib
+            collective_id=0, has_side_effects=True, vmem_limit_bytes=60 * mib
         ),
         name="model",
     )(
@@ -425,19 +460,20 @@
         functools.partial(remap_kernel, dims),
         out_shape=(
             jax.ShapeDtypeStruct((out_rows, nblk * tb), BF16),
-            jax.ShapeDtypeStruct((8, glanes), F32),
+            jax.ShapeDtypeStruct((1, glanes), F32),
         ),
-        in_specs=[vmem, hbm, smem, smem, smem],
+        in_specs=[hbm, hbm, smem, smem, smem],
         out_specs=(vmem, vmem),
         scratch_shapes=[
+            pltpu.VMEM((out_rows, n_gx * cx), BF16),
+            pltpu.VMEM((out_rows, n_gx * cx + LANES), F32),
             pltpu.VMEM((nblk, sw, tb), BF16),
-            pltpu.VMEM((nblk, sw + 2 * LANES, tb), F32),
-            dma((nblk,)),
+            dma((nblk + 1,)),
         ],
-        compiler_params=pltpu.CompilerParams(vmem_limit_bytes=30 * mib),
+        compiler_params=pltpu.CompilerParams(vmem_limit_bytes=60 * mib),
         name="remap",
     )(
-        lat.reshape(out_rows, n_gx * cx + LANES),
+        lat.reshape(out_rows, n_gx * cx),
         meridian_panel_coefficients,
         panel_starting_source_meridian,
         target_parallel_cluster,
@@ -445,16 +481,16 @@
     )
     sums = pl.pallas_call(
         functools.partial(sums_kernel, dims),
-        out_shape=jax.ShapeDtypeStruct((3, groups), F32),
+        out_shape=jax.ShapeDtypeStruct((1, glanes), F32),
         in_specs=[vmem],
         out_specs=vmem,
-        scratch_shapes=[pltpu.VMEM((total, 8, glanes), F32), dma((2,))],
+        scratch_shapes=[pltpu.VMEM((total, 1, glanes), F32), dma((2,))],
         compiler_params=pltpu.CompilerParams(
             collective_id=1, has_side_effects=True, vmem_limit_bytes=16 * mib
         ),
         name="sums",
     )(part)
-    return remapped.reshape(3, levels, trows, nblk * tb), sums
+    return remapped.reshape(3, levels, trows, nblk * tb), sums[0, : 3 * groups].reshape(3, groups)
 
 
 def solution(mesh):

time: 49.3 us -> 42.6 us (0.86)
  local copies, waits for them, and re-layouts: 7.8 us -> 3.13 us
  Pallas kernels: 40.5 us -> 38.5 us
    unnamed x23 -> x2, local copies, waits for them, and re-layouts: 6.98 us -> 0.65 us
    pallas_call x1, Pallas kernels: 8.78 us -> 7.57 us  [body(): pl.pallas_call(functools.partial(sums_kernel, dims), out_shape=jax.ShapeD...]
    pallas_call x1, Pallas kernels: 6.29 us -> 5.13 us  [body(): pl.pallas_call(functools.partial(remap_kernel, dims), out_shape=(jax.Shap...]
    reshape x1, local copies, waits for them, and re-layouts: 0.81 us -> 1.79 us  [body(): remapped.reshape(3, levels, trows, nblk * tb)]
    another operation x0 -> x1, local copies, waits for them, and re-layouts: none -> 0.66 us  [body(): sums[0, :3 * groups].reshape(3, groups)]
where the time goes in v2:
time: 42.6 us; the launch traced here: 42.3 us
  Pallas kernels  38.5 us (90%)
  local copies, waits for them, and re-layouts  3.13 us (7%)
  between operations  0.66 us (2%)
    pallas_call x1, Pallas kernels, body(): pl.pallas_call(functools.partial(model_kernel, dims), out_shape=jax.Shape...  25.8 us
    pallas_call x1, Pallas kernels, body(): pl.pallas_call(functools.partial(sums_kernel, dims), out_shape=jax.ShapeD...  7.57 us
    pallas_call x1, Pallas kernels, body(): pl.pallas_call(functools.partial(remap_kernel, dims), out_shape=(jax.Shap...  5.13 us
    reshape x1, local copies, waits for them, and re-layouts, body(): remapped.reshape(3, levels, trows, nblk * tb)  1.79 us

profile of v2, /device:TPU:0, one launch (start us, length us, event | category | flops | bytes accessed | tf_op | source)
XLA Modules:
  0.0 42.3 jit_solution(12767266377093237216)
XLA Ops:
  0.6 25.8 %model.1 = bf16[3,2,16,2048]{3,2,1,0:T(8,128)(2,1)} custom-call(f32[8,96,256]{2,1,0:T(8,128)} %temp_hbm.1, f32[8,96,256]{2,1,0:T(8,128)} %salt_hbm.1, bf16[8,96,256]{2,1,0:T(8,128)(2,1)} %zonal_hbm.1, bf16[8,96,256]{2,1,0:T(8,128)(2,1)} %merid_hbm.1, f32[8]{0:T(128)} %kappa_ref.1, s32[2]{0:T(128)} %land_ref.1, bf16[8,4,12]{2,1,0:T(4,128)(2,1)} %band_ref.1), custom_call_target="tpu_custom_call" | custom-call | tf_op jit(solution)/shard_map/model/pallas_call | solution.py:419
  26.5 5.1 %remap.1 = (bf16[96,1792]{1,0:T(8,128)(2,1)}, f32[1,128]{1,0:T(1,128)}) custom-call(bf16[96,2048]{1,0:T(8,128)(2,1)} %bitcast.1, bf16[14,512,128]{2,1,0:T(8,128)(2,1)} %panel_hbm.1, s32[14]{0:T(128)} %start_ref.1, s32[64]{0:T(128)} %cluster_ref.1, f32[64]{0:T(128)} %constant.2.clone.area_ref), custom_call_target="tpu_custom_call" | custom-call | tf_op jit(solution)/shard_map/remap/pallas_call | solution.py:459
  31.6 1.8 %reshape.11 = bf16[3,8,4,1792]{3,2,1,0:T(4,128)(2,1)} reshape(bf16[96,1792]{1,0:T(8,128)(2,1)} %get-tuple-element.4) | data formatting | bytes 688128 | tf_op jit(solution)/shard_map/reshape | solution.py:493
  33.4 0.0 copy-start
  33.4 0.7 %copy-done = f32[1,128]{1,0:T(1,128)S(1)} copy-done((f32[1,128]{1,0:T(1,128)S(1)}, f32[1,128]{1,0:T(1,128)}, u32[]{:S(2)}) %copy-start) | copy-done | bytes 536
  34.1 7.6 %sums.1 = f32[1,128]{1,0:T(1,128)S(1)} custom-call(f32[1,128]{1,0:T(1,128)S(1)} %copy-done), custom_call_target="tpu_custom_call" | custom-call | tf_op jit(solution)/shard_map/sums/pallas_call | solution.py:482
  41.7 0.7 %reshape_squeeze.3 = f32[3,8]{1,0:T(4,128)} reshape(f32[24]{0:T(128)S(1)} %slice_reduce_fusion) | data formatting | bytes 192 | tf_op jit(solution)/shard_map/reshape;squeeze | solution.py:493
  (1 shorter events, 0.0 us)
Async XLA Ops:
  33.4 0.7 %copy-start = (f32[1,128]{1,0:T(1,128)S(1)}, f32[1,128]{1,0:T(1,128)}, u32[]{:S(2)}) copy-start(f32[1,128]{1,0:T(1,128)} %get-tuple-element.5.part_ref) | copy-start | bytes 1540

commit v3 on v2

--- a/solution.py
+++ b/solution.py
@@ -279,6 +279,7 @@
     part_ref,
     lat,
     wide,
+    result,
     panel,
     sems,
 ):
@@ -340,7 +341,9 @@
         loads[j].wait()
         values = jnp.dot(window, panel[j], preferred_element_type=F32)
         squares = squares + values * values
-        out_ref[:, pl.ds(j * tb, tb)] = values.astype(BF16)
+        result[:, pl.ds(j * tb, tb)] = values
+    for i in range(3 * levels):
+        out_ref[i // levels, i % levels] = result[pl.ds(i * trows, trows), :].astype(BF16)
     weighted = jnp.sum(squares, axis=1, keepdims=True) * thick * hot
     size = levels * trows
     field = lax.div(lanes, groups)
@@ -459,7 +462,7 @@
     remapped, part = pl.pallas_call(
         functools.partial(remap_kernel, dims),
         out_shape=(
-            jax.ShapeDtypeStruct((out_rows, nblk * tb), BF16),
+            jax.ShapeDtypeStruct((3, levels, trows, nblk * tb), BF16),
             jax.ShapeDtypeStruct((1, glanes), F32),
         ),
         in_specs=[hbm, hbm, smem, smem, smem],
@@ -467,6 +470,7 @@
         scratch_shapes=[
             pltpu.VMEM((out_rows, n_gx * cx), BF16),
             pltpu.VMEM((out_rows, n_gx * cx + LANES), F32),
+            pltpu.VMEM((out_rows, nblk * tb), F32),
             pltpu.VMEM((nblk, sw, tb), BF16),
             dma((nblk + 1,)),
         ],
@@ -490,7 +494,7 @@
         ),
         name="sums",
     )(part)
-    return remapped.reshape(3, levels, trows, nblk * tb), sums[0, : 3 * groups].reshape(3, groups)
+    return remapped, sums[0, : 3 * groups].reshape(3, groups)
 
 
 def solution(mesh):

time: 42.6 us -> 40.9 us (0.960)
  local copies, waits for them, and re-layouts: 3.13 us -> 1.33 us
    reshape x1 -> x0, local copies, waits for them, and re-layouts: 1.79 us -> none  [body(): remapped.reshape(3, levels, trows, nblk * tb)]
where the time goes in v3:
time: 40.9 us; the launch traced here: 40.6 us
  Pallas kernels  38.6 us (94%)
  local copies, waits for them, and re-layouts  1.33 us (3%)
  between operations  0.66 us (2%)
    pallas_call x1, Pallas kernels, body(): pl.pallas_call(functools.partial(model_kernel, dims), out_shape=jax.Shape...  25.8 us
    pallas_call x1, Pallas kernels, body(): pl.pallas_call(functools.partial(sums_kernel, dims), out_shape=jax.ShapeD...  7.57 us
    pallas_call x1, Pallas kernels, body(): pl.pallas_call(functools.partial(remap_kernel, dims), out_shape=(jax.Shap...  5.22 us

profile of v3, /device:TPU:0, one launch (start us, length us, event | category | flops | bytes accessed | tf_op | source)
XLA Modules:
  0.0 40.6 jit_solution(2436129987466775555)
XLA Ops:
  0.6 25.8 %model.1 = bf16[3,2,16,2048]{3,2,1,0:T(8,128)(2,1)} custom-call(f32[8,96,256]{2,1,0:T(8,128)} %temp_hbm.1, f32[8,96,256]{2,1,0:T(8,128)} %salt_hbm.1, bf16[8,96,256]{2,1,0:T(8,128)(2,1)} %zonal_hbm.1, bf16[8,96,256]{2,1,0:T(8,128)(2,1)} %merid_hbm.1, f32[8]{0:T(128)} %kappa_ref.1, s32[2]{0:T(128)} %land_ref.1, bf16[8,4,12]{2,1,0:T(4,128)(2,1)} %band_ref.1), custom_call_target="tpu_custom_call" | custom-call | tf_op jit(solution)/shard_map/model/pallas_call | solution.py:422
  26.5 5.2 %remap.1 = (bf16[3,8,4,1792]{3,2,1,0:T(4,128)(2,1)}, f32[1,128]{1,0:T(1,128)}) custom-call(bf16[96,2048]{1,0:T(8,128)(2,1)} %bitcast.1, bf16[14,512,128]{2,1,0:T(8,128)(2,1)} %panel_hbm.1, s32[14]{0:T(128)} %start_ref.1, s32[64]{0:T(128)} %cluster_ref.1, f32[64]{0:T(128)} %constant.2.clone.area_ref), custom_call_target="tpu_custom_call" | custom-call | tf_op jit(solution)/shard_map/remap/pallas_call | solution.py:462
  31.7 0.0 copy-start
  31.7 0.6 %copy-done = f32[1,128]{1,0:T(1,128)S(1)} copy-done((f32[1,128]{1,0:T(1,128)S(1)}, f32[1,128]{1,0:T(1,128)}, u32[]{:S(2)}) %copy-start) | copy-done | bytes 536
  32.4 7.6 %sums.1 = f32[1,128]{1,0:T(1,128)S(1)} custom-call(f32[1,128]{1,0:T(1,128)S(1)} %copy-done), custom_call_target="tpu_custom_call" | custom-call | tf_op jit(solution)/shard_map/sums/pallas_call | solution.py:486
  39.9 0.7 %reshape_squeeze.3 = f32[3,8]{1,0:T(4,128)} reshape(f32[24]{0:T(128)S(1)} %slice_reduce_fusion) | data formatting | bytes 192 | tf_op jit(solution)/shard_map/reshape;squeeze | solution.py:497
  (1 shorter events, 0.0 us)
Async XLA Ops:
  31.7 0.7 %copy-start = (f32[1,128]{1,0:T(1,128)S(1)}, f32[1,128]{1,0:T(1,128)}, u32[]{:S(2)}) copy-start(f32[1,128]{1,0:T(1,128)} %get-tuple-element.5.part_ref) | copy-start | bytes 1540
